TPU v7x, 32 devices: a whole 2x2x4 slice. The times are simulated.
32 devices in a mesh: tm: 32 (over z, y, x, core).
Axes of the slice: x: 2, y: 2, z: 4, core: 2. Of those that a mesh axis runs over, the one named last changes fastest.
Arguments:
- field: bfloat16 [10752, 2048], P('tm'), may hold values from -52 to 52
- index: float32 [10752, 10], P('tm'), may hold values from -13 to 13
- lag_list: int32 [61], replicated, may hold values from -30 to 30, as said below
- index_offset: int32 [10], replicated, may hold values from 0 to 14, as said below
- sea_mask: int32 [2048], P('tm'), may hold values 0 or 1
Outputs:
- corr_maps: float32 [2048, 10, 61], P('tm')
Inputs may be any that keep to these rules, and one draw needn't show every extreme that they name: `lag_list`: each whole number of -30 to 30 appears once. `index_offset`: some index has the extra lead 14.
All inputs are finite; a program needn't handle non-finite values. No bound on the sum of `sea_mask` on one device may be relied on, other than what follows from the above.
Results may differ from a plain program's by a relative error of at most 0.00051.
Values may be sent and summed in bfloat16 or wider, within the bound.
A program may use at most 256 MiB of HBM per device.

v0:
```python
import jax
import jax.numpy as jnp
from jax import lax
from jax.sharding import PartitionSpec as P

MAXLAG = 30
MAXOFF = 14


def padded_2(array, sides, width):
    for axis, dim in sides:
        devices, length = (lax.axis_size(axis), array.shape[dim])
        up = [(i, (i + 1) % devices) for i in range(devices - 1)]
        down = [(j, i) for i, j in up]
        last = lax.slice_in_dim(array, length - width, length, axis=dim)
        initial = lax.slice_in_dim(array, 0, width, axis=dim)
        before = lax.ppermute(last, axis, up)
        after = lax.ppermute(initial, axis, down)
        array = jnp.concatenate([before, array, after], axis=dim)
    return array


def build_window_sums(padded, length, reach, lag_low):
    count = reach + lag_low + 1
    piece = lax.slice_in_dim(padded, 0, length + reach + lag_low, axis=0)
    windows = jnp.stack(
        [piece[reach + lag_low - j : reach + lag_low - j + length] for j in range(count)], 1
    )
    return windows.reshape(length, count * padded.shape[1])


def lag_selector(shifts, reach, lag_low):
    count = reach + lag_low + 1
    places = jnp.arange(count, dtype=jnp.int32)
    return (places[None, :, None] == (shifts + lag_low)[:, None, :]).astype(jnp.float32)


def pick_lags(accum, selector):
    kcount, count, lcount = selector.shape
    spread = accum.reshape(accum.shape[0], count, kcount)
    chosen = jnp.einsum("cjk,kjl->ckl", spread, selector, precision=lax.Precision.HIGHEST)
    return chosen.reshape(accum.shape[0], kcount * lcount)


def finish(products, first_sum, second_sum, prefix_totals, var_i, sea_mask, total_days):
    kcount, lcount = prefix_totals.shape
    mean_x = first_sum / total_days
    var_x = second_sum / total_days - mean_x * mean_x
    numer = products.reshape(-1, kcount, lcount) - mean_x[:, None, None] * prefix_totals[None]
    scale = (
        total_days * jnp.sqrt(var_x + 1e-06)[:, None, None] * jnp.sqrt(var_i + 1e-06)[None, :, None]
    )
    return numer / scale * sea_mask.astype(jnp.float32)[:, None, None]


def shards(field, index, lag_list, index_offset, sea_mask):
    t_dev = field.shape[0]
    devices = lax.axis_size("tm")
    day_count = t_dev * devices
    total_days = day_count * 1.0
    kcount = index.shape[1]
    reach = MAXLAG + MAXOFF
    shifts = lag_list[None, :] + index_offset[:, None]
    selector = lag_selector(shifts, reach, MAXLAG)
    first_i, second_i = lax.psum((jnp.sum(index, 0), jnp.sum(index * index, 0)), "tm")
    mean_i = first_i / total_days
    var_i = second_i / total_days - mean_i * mean_i
    centered = (index - mean_i).astype(jnp.bfloat16)
    padded = padded_2(centered, (("tm", 0),), reach)
    windows = build_window_sums(padded, t_dev, reach, MAXLAG)
    window_sums = jnp.sum(windows.astype(jnp.float32), 0)
    local_totals = pick_lags(window_sums[None, :], selector)[0]
    prefix_totals = lax.psum(local_totals, "tm").reshape(kcount, -1)
    spread = lax.dot_general(
        field, windows, (((0,), (0,)), ((), ())), preferred_element_type=jnp.float32
    )
    wide = field.astype(jnp.float32)
    combined = lax.psum_scatter(
        jnp.concatenate(
            [
                pick_lags(spread, selector),
                jnp.sum(wide, 0)[:, None],
                jnp.sum(wide * wide, 0)[:, None],
            ],
            1,
        ),
        "tm",
        scatter_dimension=0,
        tiled=True,
    )
    width_all = combined.shape[1] - 2
    products = combined[:, :width_all]
    return finish(
        products,
        combined[:, width_all],
        combined[:, width_all + 1],
        prefix_totals,
        var_i,
        sea_mask,
        total_days,
    )


def solution(mesh):
    return jax.shard_map(
        shards,
        mesh=mesh,
        in_specs=(P("tm", None), P("tm", None), P(), P(), P("tm")),
        out_specs=P("tm", None, None),
        check_vma=False,
    )
```

profile of v0, /device:TPU:0, one launch (start us, length us, event | category | flops | bytes accessed | tf_op | source)
XLA Modules:
  0.0 262.7 jit_solution(14230086272392308537)
XLA Ops:
  6.5 1.0 multiply_reduce_fusion
  7.5 42.0 %psum.21 = f32[10]{0:T(128)S(1)} all-reduce(f32[10]{0:T(128)S(1)} %get-tuple-element.8), channel_id=1, replica_groups=mesh['tm'=32] {'tm'}, use_global_device_ids=true, to_apply=%region_1.0 | all-reduce | flops 10 | bytes 80 | tf_op jit(solution)/shard_map/psum | solution.py:65
  49.5 0.8 subtract_convert_fusion
  50.4 1.3 collective-permute-start.1
  51.7 1.3 collective-permute-start
  53.0 0.7 add_add_fusion
  53.7 1.7 convert_reduce_fusion
  55.4 1.8 collective-permute-done
  57.3 0.1 constant_dynamic-update-slice_fusion.73
  57.4 0.1 constant_dynamic-update-slice_fusion.72
  57.5 0.1 constant_dynamic-update-slice_fusion.71
  57.6 0.1 constant_dynamic-update-slice_fusion.70
  57.7 0.1 constant_dynamic-update-slice_fusion.69
  57.7 0.1 constant_dynamic-update-slice_fusion.68
  57.8 0.1 constant_dynamic-update-slice_fusion.67
  57.9 0.1 constant_dynamic-update-slice_fusion.66
  58.0 0.1 constant_dynamic-update-slice_fusion.65
  58.1 0.1 constant_dynamic-update-slice_fusion.64
  58.2 0.1 constant_dynamic-update-slice_fusion.63
  58.3 0.1 constant_dynamic-update-slice_fusion.62
  58.3 0.1 constant_dynamic-update-slice_fusion.61
  58.4 0.1 constant_dynamic-update-slice_fusion.60
  58.5 0.1 constant_dynamic-update-slice_fusion.59
  58.6 0.1 constant_dynamic-update-slice_fusion.58
  58.7 0.1 constant_dynamic-update-slice_fusion.57
  58.8 0.1 constant_dynamic-update-slice_fusion.56
  58.9 0.1 constant_dynamic-update-slice_fusion.55
  59.0 0.1 constant_dynamic-update-slice_fusion.54
  59.0 0.1 constant_dynamic-update-slice_fusion.53
  59.1 0.1 constant_dynamic-update-slice_fusion.52
  59.2 0.1 constant_dynamic-update-slice_fusion.51
  59.3 0.1 constant_dynamic-update-slice_fusion.50
  59.4 0.1 constant_dynamic-update-slice_fusion.49
  59.5 0.1 constant_dynamic-update-slice_fusion.48
  59.6 0.1 constant_dynamic-update-slice_fusion.47
  59.6 0.1 constant_dynamic-update-slice_fusion.46
  59.7 0.1 constant_dynamic-update-slice_fusion.45
  59.8 0.8 constant_dynamic-update-slice_fusion.44
  61.3 0.1 constant_dynamic-update-slice_fusion.35
  61.4 0.1 constant_dynamic-update-slice_fusion.34
  61.5 0.1 constant_dynamic-update-slice_fusion.33
  61.8 0.1 constant_dynamic-update-slice_fusion.29
  61.9 0.1 constant_dynamic-update-slice_fusion.28
  62.0 0.1 constant_dynamic-update-slice_fusion.27
  62.3 0.1 constant_dynamic-update-slice_fusion.23
  62.4 0.1 constant_dynamic-update-slice_fusion.22
  62.5 0.1 constant_dynamic-update-slice_fusion.21
  62.6 0.1 constant_dynamic-update-slice_fusion.20
  64.4 0.4 reshape.99
  64.7 4.4 %convolution_bitcast_fusion = f32[2048,750]{0,1:T(8,128)} fusion(bf16[336,750]{0,1:T(8,128)(2,1)S(1)} %reshape.99, bf16[336,2048]{1,0:T(8,128)(2,1)S(1)} %copy-done), kind=kOutput, calls=%fused_computation.3 | convolution fusion | flops 1032192000 | bytes 8024256 | tf_op jit(solution)/shard_map/dot_general | solution.py:74
  69.2 7.7 %reshape.100 = f32[2048,75,10]{0,2,1:T(8,128)} reshape(f32[2048,750]{0,1:T(8,128)} %convolution_bitcast_fusion) | data formatting | bytes 12288000 | tf_op jit(solution)/shard_map/reshape | solution.py:40
  76.8 12.8 %fusion.2 = f32[2048,10,61]{0,2,1:T(8,128)} fusion(f32[2048,75,10]{0,2,1:T(8,128)} %reshape.100, s32[10,61]{1,0:T(8,128)S(1)} %add_add_fusion), kind=kOutput, calls=%fused_computation.4 | convolution fusion | flops 1124397696 | bytes 11143560 | tf_op jit(solution)/shard_map/cjk,kjl->ckl/dot_general | solution.py:41
  89.6 4.9 %reshape.101 = f32[2048,610]{0,1:T(8,128)} reshape(f32[2048,10,61]{0,2,1:T(8,128)} %fusion.2) | data formatting | bytes 9994240 | tf_op jit(solution)/shard_map/reshape | solution.py:42
  94.5 5.3 %pad_maximum_fusion = f32[2048,612]{0,1:T(8,128)} fusion(f32[2048,1]{0,1:T(1,128)S(1)} %bitcast.334, f32[2048,1]{0,1:T(1,128)S(1)} %bitcast.333, f32[2048,610]{0,1:T(8,128)} %reshape.101), kind=kLoop, calls=%fused_computation.2 | loop fusion | flops 2506752 | bytes 10027008 | tf_op jit(solution)/shard_map/concatenate | solution.py:79
  99.9 5.9 %copy.13 = f32[2048,612]{1,0:T(8,128)} copy(f32[2048,612]{0,1:T(8,128)} %pad_maximum_fusion) | data formatting | bytes 10027008
  105.8 0.6 copy-done.1
  106.4 0.2 convert_reduce_fusion.1
  106.7 0.4 fusion.6
  107.1 43.1 %all-reduce = (f32[10]{0:T(128)S(1)}, f32[10,61]{1,0:T(8,128)S(1)}) all-reduce(f32[10]{0:T(128)S(1)} %get-tuple-element.7, f32[10,61]{1,0:T(8,128)S(1)} %bitcast.335), channel_id=1, replica_groups=mesh['tm'=32] {'tm'}, use_global_device_ids=true, to_apply=%region_8.0 | all-reduce | flops 620 | bytes 4960 | tf_op jit(solution)/shard_map/psum | solution.py:65
  150.2 102.3 %reduce-scatter.4.cloned.1.call-done = f32[64,612]{1,0:T(8,128)} async-done(((f32[2048,612]{1,0:T(8,128)}), f32[64,612]{1,0:T(8,128)}) %reduce-scatter.4.cloned.1.call-update) | async-done | bytes 156688
  252.5 0.9 slice_multiply_fusion.1
  253.6 1.1 copy.15
  254.8 0.2 divide_multiply_fusion
  254.9 0.9 copy.10
  (52 shorter events, 3.4 us)
Async XLA Ops:
  6.5 58.2 %copy-start = (bf16[336,2048]{1,0:T(8,128)(2,1)S(1)}, bf16[336,2048]{1,0:T(8,128)(2,1)}, u32[]{:S(2)}) copy-start(bf16[336,2048]{1,0:T(8,128)(2,1)} %param.5) | copy-start | bytes 4128772
  6.5 246.0 %reduce-scatter.4.cloned.1.call-start = ((), (), s32[]{:S(2)}) async-start(), calls=%async_computation.1 | async-start | bytes 5406720
  50.4 10.3 %collective-permute-start.1 = (bf16[44,10]{0,1:T(8,128)(2,1)S(1)}, bf16[44,10]{0,1:T(8,128)(2,1)S(1)}, u32[]{:S(2)}, u32[]{:S(2)}) collective-permute-start(bf16[44,10]{0,1:T(8,128)(2,1)S(1)} %get-tuple-element.13), channel_id=1, source_target_pairs={{0,1},{1,2},{2,3},{3,4},{4,5},{5,6},{6,7},{7,8},{8,9},{9,10},{10,1... | collective-permute-start | bytes 2648 | tf_op jit(solution)/shard_map/ppermute | solution.py:17
  51.7 5.6 %collective-permute-start = (bf16[44,10]{0,1:T(8,128)(2,1)S(1)}, bf16[44,10]{0,1:T(8,128)(2,1)S(1)}, u32[]{:S(2)}, u32[]{:S(2)}) collective-permute-start(bf16[44,10]{0,1:T(8,128)(2,1)S(1)} %get-tuple-element.14), channel_id=1, source_target_pairs={{1,0},{2,1},{3,2},{4,3},{5,4},{6,5},{7,6},{8,7},{9,8},{10,9},{11,1... | collective-permute-start | bytes 2648 | tf_op jit(solution)/shard_map/ppermute | solution.py:18
  105.7 0.7 copy-start.1
Sparse Core Ops, SparseCore 0:
  105.9 146.5 reduce-scatter.3
where the time goes:
time: 264 us; the launch traced here: 263 us
  waiting for transfers between devices  104 us (39%)
  blocking collectives  85.1 us (32%)
  local copies, waits for them, and re-layouts  21.8 us (8%)
  other arithmetic  18.1 us (7%)
  matrix products  17.6 us (7%)
  between operations  13.5 us (5%)
    unnamed x2, waiting for transfers between devices  102 us
    psum x2, blocking collectives, shards(): lax.psum((jnp.sum(index, 0), jnp.sum(index * index, 0)), 'tm')  85.1 us
    dot_general x2, matrix products, pick_lags(): jnp.einsum('cjk,kjl->ckl', spread, selector, precision=lax.Precision.HIGH...  13.2 us
    unnamed x8, local copies, waits for them, and re-layouts  7.73 us
    reshape x1, local copies, waits for them, and re-layouts, pick_lags(): spread = accum.reshape(accum.shape[0], count, kcount)  7.69 us
    unnamed x74, other arithmetic  7 us
    concatenate x1, other arithmetic, shards(): jnp.concatenate([pick_lags(spread, selector), jnp.sum(wide, 0)[:, None],...  5.35 us
  transfers between devices with their start and end apart: 3, of which 2 were waited for; matrix products, arithmetic and copies ran while one was open for 3% of the time, Pallas kernels for 0%

commit v1 on v0

v1 whole, which is shorter than its diff:
```python
import functools

import jax
import jax.numpy as jnp
from jax import lax
from jax.experimental import pallas as pl
from jax.experimental.pallas import tpu as pltpu
from jax.sharding import PartitionSpec as P

MAXLAG = 30
MAXOFF = 14
PLACES = 2 * MAXLAG + MAXOFF + 1
MESH = pl.DeviceIdType.MESH


def round_up(value, unit):
    return -(-value // unit) * unit


def kernel(
    sizes,
    field_ref,
    idx_ref,
    acc_out,
    stat_out,
    tot_out,
    var_out,
    recv,
    idx_all,
    win,
    acc,
    acc_in,
    field_send,
    field_recv,
    one_send,
    one_recv,
    two_send,
    two_recv,
    last_send,
    last_recv,
    own_sem,
):
    devices, t_dev, kcount, kpad, rows, low = sizes
    chips = devices // 2
    high = chips // low
    lanes = idx_ref.shape[1]
    wide = lanes + 128
    me = lax.axis_index("tm")
    chip = lax.div(me, 2)
    core = lax.rem(me, 2)
    hi = lax.div(chip, low)
    lo = lax.rem(chip, low)
    partner = chip * 2 + (1 - core)
    cells = recv.shape[2]

    def slot_of(device):
        at = lax.div(device, 2)
        return (lax.rem(device, 2) * low + lax.rem(at, low)) * high + lax.div(at, low)

    def block(at):
        return field_ref.at[:, pl.ds(pl.multiple_of(at * cells, cells), cells)]

    my_slot = slot_of(me)

    def one_copy(step):
        to = lax.rem(hi + step, high)
        return pltpu.make_async_remote_copy(
            src_ref=idx_ref,
            dst_ref=idx_all.at[my_slot],
            send_sem=one_send.at[step],
            recv_sem=one_recv.at[step],
            device_id=((to * low + lo) * 2 + core,),
            device_id_type=MESH,
        )

    def two_copy(step):
        to = lax.rem(lo + step, low)
        part = idx_all.at[pl.ds((core * low + lo) * high, high)]
        return pltpu.make_async_remote_copy(
            src_ref=part,
            dst_ref=part,
            send_sem=two_send.at[step],
            recv_sem=two_recv.at[step],
            device_id=((hi * low + to) * 2 + core,),
            device_id_type=MESH,
        )

    def last_copy():
        part = idx_all.at[pl.ds(core * chips, chips)]
        return pltpu.make_async_remote_copy(
            src_ref=part,
            dst_ref=part,
            send_sem=last_send.at[0],
            recv_sem=last_recv.at[0],
            device_id=(partner,),
            device_id_type=MESH,
        )

    def field_copy(step):
        to = lax.rem(chip + step, chips)
        return pltpu.make_async_remote_copy(
            src_ref=block(to),
            dst_ref=recv.at[step],
            send_sem=field_send.at[step],
            recv_sem=field_recv.at[step],
            device_id=(to * 2 + core,),
            device_id_type=MESH,
        )

    def each(low_step, high_step, act):
        def body(step, carry):
            act(step)
            return carry

        lax.fori_loop(low_step, high_step, body, 0)

    own_idx = pltpu.make_async_copy(idx_ref, idx_all.at[my_slot], own_sem.at[0])
    own_field = pltpu.make_async_copy(block(chip), recv.at[0], own_sem.at[1])
    own_idx.start()
    own_field.start()
    each(1, high, lambda s: one_copy(s).start())
    each(1, chips, lambda s: field_copy(s).start())
    own_idx.wait()
    own_field.wait()
    each(1, high, lambda s: one_copy(s).wait())
    each(1, low, lambda s: two_copy(s).start())
    each(1, low, lambda s: two_copy(s).wait())
    last_copy().start()
    last_copy().wait()

    total_days = devices * t_dev * 1.0

    def sum_body(at, carry):
        first, second = carry
        value = idx_all[at]
        return first + value, second + value * value

    zero = jnp.zeros((kpad, lanes), jnp.float32)
    first, second = lax.fori_loop(0, devices, sum_body, (zero, zero))
    mean = jnp.sum(first, 1, keepdims=True) / total_days
    var = jnp.sum(second, 1, keepdims=True) / total_days - mean * mean
    var_out[...] = jnp.broadcast_to(var, (kpad, 128))
    valid = lax.broadcasted_iota(jnp.int32, (kpad, lanes), 1) < t_dev

    def center_body(at, carry):
        value = (idx_all[at] - mean).astype(jnp.bfloat16).astype(jnp.float32)
        value = jnp.where(valid, value, 0.0)
        idx_all[at] = value
        return carry + value

    centered_sum = jnp.sum(lax.fori_loop(0, devices, center_body, zero), 1, keepdims=True)
    day = lax.broadcasted_iota(jnp.int32, (lanes, 128), 0)
    shift = lax.broadcasted_iota(jnp.int32, (lanes, 128), 1) - MAXLAG
    late = jnp.where((day >= t_dev - shift) & (day < t_dev), 1.0, 0.0).astype(jnp.bfloat16)
    early = jnp.where(day < -shift, 1.0, 0.0).astype(jnp.bfloat16)
    dropped = jnp.dot(
        idx_all[slot_of(devices - 1)].astype(jnp.bfloat16),
        late,
        preferred_element_type=jnp.float32,
    ) + jnp.dot(
        idx_all[0].astype(jnp.bfloat16), early, preferred_element_type=jnp.float32
    )
    tot_out[...] = centered_sum - dropped

    acc[...] = jnp.zeros_like(acc)
    place = lax.broadcasted_iota(jnp.int32, (kpad, wide), 1)
    tail = jnp.zeros((kpad, 128), jnp.float32)
    reach = 64

    def source_body(step, carry):
        from_chip = lax.rem(chip - step + chips, chips)
        device = from_chip * 2 + core
        before = idx_all[slot_of(jnp.maximum(device - 1, 0))]
        after = idx_all[slot_of(jnp.minimum(device + 1, devices - 1))]
        before = before * jnp.where(device > 0, 1.0, 0.0)
        after = after * jnp.where(device < devices - 1, 1.0, 0.0)
        here = jnp.concatenate([idx_all[slot_of(device)], tail], 1)
        before = jnp.concatenate([before, tail], 1)
        after = jnp.concatenate([after, tail], 1)
        left = pltpu.roll(before, (reach - t_dev) % wide, 1)
        mid = pltpu.roll(here, reach, 1)
        right = pltpu.roll(after, reach + t_dev, 1)
        ext = jnp.where(place < reach, left, jnp.where(place < reach + t_dev, mid, right))
        for k in range(kcount):
            line = jnp.broadcast_to(ext[k : k + 1], (rows, wide))
            turned = pltpu.roll(line, wide - reach - MAXLAG, 1, stride=1, stride_axis=0)
            win[k * rows : (k + 1) * rows, :] = turned[:, :lanes].astype(jnp.bfloat16)

        @pl.when(step > 0)
        def _():
            field_copy(step).wait()

        got = recv[step]
        acc[0 : kcount * rows, :] += jnp.dot(
            win[:, :t_dev], got, preferred_element_type=jnp.float32
        )
        value = got.astype(jnp.float32)
        acc[kcount * rows : kcount * rows + 1, :] += jnp.sum(value, 0, keepdims=True)
        acc[kcount * rows + 1 : kcount * rows + 2, :] += jnp.sum(value * value, 0, keepdims=True)
        return carry

    lax.fori_loop(0, chips, source_body, 0)
    swap = pltpu.make_async_remote_copy(
        src_ref=acc,
        dst_ref=acc_in,
        send_sem=last_send.at[1],
        recv_sem=last_recv.at[1],
        device_id=(partner,),
        device_id_type=MESH,
    )
    swap.start()
    swap.wait()
    count = kcount * rows
    acc_out[...] = acc[0:count, :] + acc_in[0:count, :]
    stat_out[...] = acc[count:, :] + acc_in[count:, :]


def gather_products(field, index_rows, devices, kcount):
    t_dev, cells_all = field.shape
    kpad, lanes = index_rows.shape
    chips = devices // 2
    cells = cells_all // chips
    rows = round_up(PLACES, 16)
    low = 1
    while low * low < chips:
        low *= 2
    high = chips // low
    sizes = (devices, t_dev, kcount, kpad, rows, low)
    dma = pltpu.SemaphoreType.DMA
    f32 = jnp.float32
    return pl.pallas_call(
        functools.partial(kernel, sizes),
        out_shape=(
            jax.ShapeDtypeStruct((kcount * rows, cells), f32),
            jax.ShapeDtypeStruct((8, cells), f32),
            jax.ShapeDtypeStruct((kpad, 128), f32),
            jax.ShapeDtypeStruct((kpad, 128), f32),
        ),
        in_specs=[pl.BlockSpec(memory_space=pltpu.VMEM)] * 2,
        out_specs=(pl.BlockSpec(memory_space=pltpu.VMEM),) * 4,
        scratch_shapes=[
            pltpu.VMEM((chips, t_dev, cells), jnp.bfloat16),
            pltpu.VMEM((devices, kpad, lanes), f32),
            pltpu.VMEM((kcount * rows, lanes), jnp.bfloat16),
            pltpu.VMEM((kcount * rows + 8, cells), f32),
            pltpu.VMEM((kcount * rows + 8, cells), f32),
            dma((chips,)),
            dma((chips,)),
            dma((high,)),
            dma((high,)),
            dma((low,)),
            dma((low,)),
            dma((2,)),
            dma((2,)),
            dma((2,)),
        ],
        compiler_params=pltpu.CompilerParams(
            has_side_effects=True, vmem_limit_bytes=56 * 1024 * 1024
        ),
    )(field, index_rows)


def shards(field, index, lag_list, index_offset, sea_mask):
    t_dev = field.shape[0]
    devices = lax.axis_size("tm")
    total_days = t_dev * devices * 1.0
    kcount = index.shape[1]
    cell_count = sea_mask.shape[0]
    kpad = round_up(kcount, 16)
    lanes = round_up(t_dev, 128)
    rows = round_up(PLACES, 16)
    index_rows = jnp.pad(index.T, ((0, kpad - kcount), (0, lanes - t_dev)))
    products, stats, totals, var_i = gather_products(field, index_rows, devices, kcount)
    begin = lax.rem(lax.axis_index("tm"), 2) * cell_count
    products = lax.dynamic_slice_in_dim(products, begin, cell_count, 1)
    stats = lax.dynamic_slice_in_dim(stats, begin, cell_count, 1)
    shifts = lag_list[None, :] + index_offset[:, None]
    places = jnp.arange(rows, dtype=jnp.int32)
    selector = (places[None, :, None] == (shifts + MAXLAG)[:, None, :]).astype(jnp.float32)
    mean_x = stats[0] / total_days
    var_x = stats[1] / total_days - mean_x * mean_x
    spread = products.reshape(kcount, rows, cell_count)
    spread = spread - mean_x[None, None, :] * totals[:kcount, :rows, None]
    inner = jnp.sqrt(var_x + 1e-06)[None, None, :]
    outer = jnp.sqrt(var_i[:kcount, 0] + 1e-06)[:, None, None]
    spread = spread / (total_days * inner * outer)
    spread = spread * sea_mask.astype(jnp.float32)[None, None, :]
    return jnp.einsum("kjc,kjl->ckl", spread, selector, precision=lax.Precision.HIGHEST)


def solution(mesh):
    return jax.shard_map(
        shards,
        mesh=mesh,
        in_specs=(P("tm", None), P("tm", None), P(), P(), P("tm")),
        out_specs=P("tm", None, None),
        check_vma=False,
    )
```

time: 264 us -> 54.9 us (0.21)
  the two profiles are of different devices: /device:TPU:0 before, /device:TPU:9 now
where the time goes in v1:
time: 54.9 us; the launch traced here: 54.7 us
  Pallas kernels  49.6 us (90%)
  local copies, waits for them, and re-layouts  3.84 us (7%)
  other arithmetic  0.63 us (1%)
    pallas_call x1, Pallas kernels, gather_products(): pl.pallas_call(functools.partial(kernel, sizes), out_shape=(jax.ShapeDtyp...  49.6 us
    pad x1, local copies, waits for them, and re-layouts, shards(): index_rows = jnp.pad(index.T, ((0, kpad - kcount), (0, lanes - t_dev)))  1.35 us
    dynamic_slice x1, local copies, waits for them, and re-layouts, shards(): products = lax.dynamic_slice_in_dim(products, begin, cell_count, 1)  1.19 us

profile of v1, /device:TPU:9, one launch (start us, length us, event | category | flops | bytes accessed | tf_op | source)
XLA Modules:
  0.0 54.7 jit_solution(6587753573743855043)
XLA Ops:
  0.0 1.3 %pad.4.idx_ref = f32[16,384]{1,0:T(8,128)} pad(f32[10,336]{1,0:T(8,128)} %bitcast.18, f32[]{:T(128)} %constant.6.clone.1), padding=0_6x0_48 | pad | bytes 38020 | tf_op jit(solution)/shard_map/jit(_pad)/pad | solution.py:272
  1.4 0.0 copy-start.5
  1.4 49.6 %shard_map.55 = (f32[800,128]{1,0:T(8,128)}, f32[8,128]{1,0:T(8,128)}, f32[16,128]{1,0:T(8,128)}, f32[16,128]{1,0:T(8,128)}) custom-call(bf16[336,2048]{1,0:T(8,128)(2,1)} %field_ref.1, f32[16,384]{1,0:T(8,128)} %pad.4.idx_ref), custom_call_target="tpu_custom_call" | custom-call | tf_op jit(solution)/shard_map/pallas_call | solution.py:231
  51.0 0.0 copy-start.2
  51.0 0.0 copy-start.1
  51.0 0.0 copy-start
  51.0 0.0 copy-start.3
  51.0 0.0 copy-start.4
  51.0 1.2 %constant_dynamic-slice_fusion.1 = f32[800,64]{1,0:T(8,128)S(1)} fusion(f32[800,128]{1,0:T(8,128)} %get-tuple-element.9, s32[]{:T(128)S(6)} %select_n.4), kind=kLoop, calls=%fused_computation.13 | loop fusion | bytes 409604 | tf_op jit(solution)/shard_map/dynamic_slice | solution.py:275
  52.2 0.3 copy.10
  52.5 0.0 copy-done.2
  52.5 0.1 constant_dynamic-slice_fusion
  52.6 0.0 copy-done.1
  52.6 0.1 sqrt_reduce_fusion
  52.7 0.1 broadcast_multiply_fusion
  52.8 0.0 copy-done.5
  52.8 0.0 copy-done
  52.8 0.3 divide_multiply_fusion
  53.2 0.0 copy-done.3
  53.2 0.0 copy-done.4
  53.2 0.1 add_add_fusion
  53.3 0.5 convolution_bitcast_fusion
  53.8 0.9 %copy.9 = f32[64,10,61]{2,0,1:T(8,128)} copy(f32[64,10,61]{0,2,1:T(8,128)S(1)} %convolution_bitcast_fusion) | data formatting | bytes 312320 | tf_op jit(solution)/shard_map/kjc,kjl->ckl/transpose | solution.py:288
  (3 shorter events, 0.0 us)
Async XLA Ops:
  1.4 51.5 %copy-start.5 = (s32[64]{0:T(128)S(1)}, s32[64]{0:T(128)}, u32[]{:S(2)}) copy-start(s32[64]{0:T(128)} %param.9) | copy-start | bytes 772
  51.0 1.6 %copy-start.2 = (f32[8,128]{1,0:T(8,128)S(1)}, f32[8,128]{1,0:T(8,128)}, u32[]{:S(2)}) copy-start(f32[8,128]{1,0:T(8,128)} %get-tuple-element.10) | copy-start | bytes 12292
  51.0 1.6 %copy-start.1 = (f32[16,128]{1,0:T(8,128)S(1)}, f32[16,128]{1,0:T(8,128)}, u32[]{:S(2)}) copy-start(f32[16,128]{1,0:T(8,128)} %get-tuple-element.12) | copy-start | bytes 24580
  51.0 1.9 %copy-start = (f32[16,128]{1,0:T(8,128)S(1)}, f32[16,128]{1,0:T(8,128)}, u32[]{:S(2)}) copy-start(f32[16,128]{1,0:T(8,128)} %get-tuple-element.11) | copy-start | bytes 24580
  51.0 2.2 %copy-start.3 = (s32[10]{0:T(128)S(1)}, s32[10]{0:T(128)}, u32[]{:S(2)}) copy-start(s32[10]{0:T(128)} %param.8) | copy-start | bytes 124
  51.0 2.2 %copy-start.4 = (s32[61]{0:T(128)S(1)}, s32[61]{0:T(128)}, u32[]{:S(2)}) copy-start(s32[61]{0:T(128)} %param.7) | copy-start | bytes 736

commit v2 on v1

--- a/solution.py
+++ b/solution.py
@@ -19,12 +19,14 @@
 
 def kernel(
     sizes,
+    field_hbm,
+    index_ref,
+    lag_ref,
+    offset_ref,
+    mask_ref,
+    out_ref,
     field_ref,
     idx_ref,
-    acc_out,
-    stat_out,
-    tot_out,
-    var_out,
     recv,
     idx_all,
     win,
@@ -53,6 +55,13 @@
     partner = chip * 2 + (1 - core)
     cells = recv.shape[2]
 
+    def across(step):
+        other, bit = 0, 1
+        while bit < chips:
+            flip = lax.rem(lax.div(chip, bit) + lax.div(step, bit), 2)
+            other, bit = other + flip * bit, bit * 2
+        return other
+
     def slot_of(device):
         at = lax.div(device, 2)
         return (lax.rem(device, 2) * low + lax.rem(at, low)) * high + lax.div(at, low)
@@ -97,7 +106,7 @@
         )
 
     def field_copy(step):
-        to = lax.rem(chip + step, chips)
+        to = across(step)
         return pltpu.make_async_remote_copy(
             src_ref=block(to),
             dst_ref=recv.at[step],
@@ -114,6 +123,20 @@
 
         lax.fori_loop(low_step, high_step, body, 0)
 
+    load = pltpu.make_async_copy(field_hbm, field_ref, own_sem.at[2])
+    load.start()
+    barrier = pltpu.get_barrier_semaphore()
+
+    def greet(device):
+        pl.semaphore_signal(barrier, inc=1, device_id=(device,), device_id_type=MESH)
+
+    each(1, chips, lambda s: greet(across(s) * 2 + core))
+    greet(partner)
+    idx_ref[...] = jnp.zeros_like(idx_ref)
+    idx_ref[0:kcount, 0:t_dev] = index_ref[...]
+    acc[...] = jnp.zeros_like(acc)
+    pl.semaphore_wait(barrier, chips)
+    load.wait()
     own_idx = pltpu.make_async_copy(idx_ref, idx_all.at[my_slot], own_sem.at[0])
     own_field = pltpu.make_async_copy(block(chip), recv.at[0], own_sem.at[1])
     own_idx.start()
@@ -139,7 +162,6 @@
     first, second = lax.fori_loop(0, devices, sum_body, (zero, zero))
     mean = jnp.sum(first, 1, keepdims=True) / total_days
     var = jnp.sum(second, 1, keepdims=True) / total_days - mean * mean
-    var_out[...] = jnp.broadcast_to(var, (kpad, 128))
     valid = lax.broadcasted_iota(jnp.int32, (kpad, lanes), 1) < t_dev
 
     def center_body(at, carry):
@@ -160,16 +182,14 @@
     ) + jnp.dot(
         idx_all[0].astype(jnp.bfloat16), early, preferred_element_type=jnp.float32
     )
-    tot_out[...] = centered_sum - dropped
-
-    acc[...] = jnp.zeros_like(acc)
+    totals = jnp.transpose(centered_sum - dropped)
+
     place = lax.broadcasted_iota(jnp.int32, (kpad, wide), 1)
     tail = jnp.zeros((kpad, 128), jnp.float32)
     reach = 64
 
-    def source_body(step, carry):
-        from_chip = lax.rem(chip - step + chips, chips)
-        device = from_chip * 2 + core
+    def window_body(step, carry):
+        device = across(step) * 2 + core
         before = idx_all[slot_of(jnp.maximum(device - 1, 0))]
         after = idx_all[slot_of(jnp.minimum(device + 1, devices - 1))]
         before = before * jnp.where(device > 0, 1.0, 0.0)
@@ -184,21 +204,24 @@
         for k in range(kcount):
             line = jnp.broadcast_to(ext[k : k + 1], (rows, wide))
             turned = pltpu.roll(line, wide - reach - MAXLAG, 1, stride=1, stride_axis=0)
-            win[k * rows : (k + 1) * rows, :] = turned[:, :lanes].astype(jnp.bfloat16)
-
+            win[step, k * rows : (k + 1) * rows, :] = turned[:, :lanes].astype(jnp.bfloat16)
+        return carry
+
+    def source_body(step, carry):
         @pl.when(step > 0)
         def _():
             field_copy(step).wait()
 
         got = recv[step]
         acc[0 : kcount * rows, :] += jnp.dot(
-            win[:, :t_dev], got, preferred_element_type=jnp.float32
+            win[step, :, :t_dev], got, preferred_element_type=jnp.float32
         )
         value = got.astype(jnp.float32)
         acc[kcount * rows : kcount * rows + 1, :] += jnp.sum(value, 0, keepdims=True)
         acc[kcount * rows + 1 : kcount * rows + 2, :] += jnp.sum(value * value, 0, keepdims=True)
         return carry
 
+    lax.fori_loop(0, chips, window_body, 0)
     lax.fori_loop(0, chips, source_body, 0)
     swap = pltpu.make_async_remote_copy(
         src_ref=acc,
@@ -211,16 +234,41 @@
     swap.start()
     swap.wait()
     count = kcount * rows
-    acc_out[...] = acc[0:count, :] + acc_in[0:count, :]
-    stat_out[...] = acc[count:, :] + acc_in[count:, :]
-
-
-def gather_products(field, index_rows, devices, kcount):
+    half = cells // 2
+
+    def mine(begin, end):
+        total = acc[begin:end, :] + acc_in[begin:end, :]
+        return jnp.where(core == 0, total[:, :half], total[:, half:])
+
+    mean_x = mine(count, count + 1) / total_days
+    var_x = mine(count + 1, count + 2) / total_days - mean_x * mean_x
+    inner = total_days * jnp.sqrt(var_x + 1e-06)
+    mask = mask_ref[...].astype(jnp.float32)
+    outer = jnp.sqrt(var + 1e-06)
+    lag = lag_ref[...]
+    row = lax.broadcasted_iota(jnp.int32, (rows, lag.shape[1]), 0)
+    for k in range(kcount):
+        numer = mine(k * rows, (k + 1) * rows) - mean_x * totals[0:rows, k : k + 1]
+        value = numer / (inner * outer[k : k + 1]) * mask
+        chosen = jnp.where(row == lag + (offset_ref[k] + MAXLAG), 1.0, 0.0)
+        out_ref[k] = lax.dot_general(
+            value,
+            chosen,
+            (((0,), (0,)), ((), ())),
+            precision=lax.Precision.HIGHEST,
+            preferred_element_type=jnp.float32,
+        )
+
+
+def shards(field, index, lag_list, index_offset, sea_mask):
     t_dev, cells_all = field.shape
-    kpad, lanes = index_rows.shape
+    devices = lax.axis_size("tm")
+    kcount = index.shape[1]
+    kpad = round_up(kcount, 16)
+    lanes = round_up(t_dev, 128)
+    rows = round_up(PLACES, 16)
     chips = devices // 2
     cells = cells_all // chips
-    rows = round_up(PLACES, 16)
     low = 1
     while low * low < chips:
         low *= 2
@@ -228,20 +276,24 @@
     sizes = (devices, t_dev, kcount, kpad, rows, low)
     dma = pltpu.SemaphoreType.DMA
     f32 = jnp.float32
-    return pl.pallas_call(
+    vmem = pl.BlockSpec(memory_space=pltpu.VMEM)
+    maps = pl.pallas_call(
         functools.partial(kernel, sizes),
-        out_shape=(
-            jax.ShapeDtypeStruct((kcount * rows, cells), f32),
-            jax.ShapeDtypeStruct((8, cells), f32),
-            jax.ShapeDtypeStruct((kpad, 128), f32),
-            jax.ShapeDtypeStruct((kpad, 128), f32),
-        ),
-        in_specs=[pl.BlockSpec(memory_space=pltpu.VMEM)] * 2,
-        out_specs=(pl.BlockSpec(memory_space=pltpu.VMEM),) * 4,
+        out_shape=jax.ShapeDtypeStruct((kcount, cells // 2, lag_list.shape[0]), f32),
+        in_specs=[
+            pl.BlockSpec(memory_space=pl.ANY),
+            vmem,
+            vmem,
+            pl.BlockSpec(memory_space=pltpu.SMEM),
+            vmem,
+        ],
+        out_specs=vmem,
         scratch_shapes=[
+            pltpu.VMEM((t_dev, cells_all), jnp.bfloat16),
+            pltpu.VMEM((kpad, lanes), f32),
             pltpu.VMEM((chips, t_dev, cells), jnp.bfloat16),
             pltpu.VMEM((devices, kpad, lanes), f32),
-            pltpu.VMEM((kcount * rows, lanes), jnp.bfloat16),
+            pltpu.VMEM((chips, kcount * rows, lanes), jnp.bfloat16),
             pltpu.VMEM((kcount * rows + 8, cells), f32),
             pltpu.VMEM((kcount * rows + 8, cells), f32),
             dma((chips,)),
@@ -252,40 +304,13 @@
             dma((low,)),
             dma((2,)),
             dma((2,)),
-            dma((2,)),
+            dma((3,)),
         ],
         compiler_params=pltpu.CompilerParams(
-            has_side_effects=True, vmem_limit_bytes=56 * 1024 * 1024
+            collective_id=0, has_side_effects=True, vmem_limit_bytes=60 * 1024 * 1024
         ),
-    )(field, index_rows)
-
-
-def shards(field, index, lag_list, index_offset, sea_mask):
-    t_dev = field.shape[0]
-    devices = lax.axis_size("tm")
-    total_days = t_dev * devices * 1.0
-    kcount = index.shape[1]
-    cell_count = sea_mask.shape[0]
-    kpad = round_up(kcount, 16)
-    lanes = round_up(t_dev, 128)
-    rows = round_up(PLACES, 16)
-    index_rows = jnp.pad(index.T, ((0, kpad - kcount), (0, lanes - t_dev)))
-    products, stats, totals, var_i = gather_products(field, index_rows, devices, kcount)
-    begin = lax.rem(lax.axis_index("tm"), 2) * cell_count
-    products = lax.dynamic_slice_in_dim(products, begin, cell_count, 1)
-    stats = lax.dynamic_slice_in_dim(stats, begin, cell_count, 1)
-    shifts = lag_list[None, :] + index_offset[:, None]
-    places = jnp.arange(rows, dtype=jnp.int32)
-    selector = (places[None, :, None] == (shifts + MAXLAG)[:, None, :]).astype(jnp.float32)
-    mean_x = stats[0] / total_days
-    var_x = stats[1] / total_days - mean_x * mean_x
-    spread = products.reshape(kcount, rows, cell_count)
-    spread = spread - mean_x[None, None, :] * totals[:kcount, :rows, None]
-    inner = jnp.sqrt(var_x + 1e-06)[None, None, :]
-    outer = jnp.sqrt(var_i[:kcount, 0] + 1e-06)[:, None, None]
-    spread = spread / (total_days * inner * outer)
-    spread = spread * sea_mask.astype(jnp.float32)[None, None, :]
-    return jnp.einsum("kjc,kjl->ckl", spread, selector, precision=lax.Precision.HIGHEST)
+    )(field, index.T, lag_list[None, :], index_offset, sea_mask[None, :])
+    return jnp.transpose(maps, (1, 0, 2))
 
 
 def solution(mesh):

time: 54.9 us -> 44.3 us (0.81)
  Pallas kernels: 49.6 us -> 42.3 us
  local copies, waits for them, and re-layouts: 3.84 us -> 1.72 us
  other arithmetic: 0.63 us -> 0 us
    pallas_call x1, Pallas kernels: 49.6 us -> 42.3 us  [shards(): pl.pallas_call(functools.partial(kernel, sizes), out_shape=jax.ShapeDtype...]
    unnamed x12 -> x1, local copies, waits for them, and re-layouts: 0.03 us -> 1.72 us
    pad x1 -> x0, local copies, waits for them, and re-layouts: 1.35 us -> none  [shards(): index_rows = jnp.pad(index.T, ((0, kpad - kcount), (0, lanes - t_dev)))]
    dynamic_slice x2 -> x0, local copies, waits for them, and re-layouts: 1.26 us -> none  [the longest x1 1.19 us: shards(): products = lax.dynamic_slice_in_dim(products, begin, cell_count, 1)]
    transpose x1 -> x0, local copies, waits for them, and re-layouts: 0.89 us -> none  [shards(): jnp.einsum('kjc,kjl->ckl', spread, selector, precision=lax.Precision.HIGH...]
where the time goes in v2:
time: 44.3 us; the launch traced here: 44.1 us
  Pallas kernels  42.3 us (95%)
  local copies, waits for them, and re-layouts  1.72 us (4%)
    pallas_call x1, Pallas kernels, shards(): pl.pallas_call(functools.partial(kernel, sizes), out_shape=jax.ShapeDtype...  42.3 us
    unnamed x1, local copies, waits for them, and re-layouts  1.72 us

profile of v2, /device:TPU:9, one launch (start us, length us, event | category | flops | bytes accessed | tf_op | source)
XLA Modules:
  0.0 44.1 jit_solution(17524189942518513195)
XLA Ops:
  0.0 42.3 %shard_map.55 = f32[10,64,61]{2,1,0:T(8,128)} custom-call(bf16[336,2048]{1,0:T(8,128)(2,1)} %field_hbm.1, f32[10,336]{1,0:T(8,128)} %bitcast.5, s32[1,61]{1,0:T(1,128)} %bitcast.6, s32[10]{0:T(128)} %offset_ref.1, s32[1,64]{1,0:T(1,128)} %bitcast.7), custom_call_target="tpu_custom_call" | custom-call | tf_op jit(solution)/shard_map/pallas_call | solution.py:280
  42.3 1.7 %copy.7 = f32[64,10,61]{2,0,1:T(8,128)} copy(f32[64,10,61]{2,0,1:T(8,128)} %bitcast.4) | data formatting | bytes 312320

commit v3 on v2

--- a/solution.py
+++ b/solution.py
@@ -182,7 +182,8 @@
     ) + jnp.dot(
         idx_all[0].astype(jnp.bfloat16), early, preferred_element_type=jnp.float32
     )
-    totals = jnp.transpose(centered_sum - dropped)
+    fill = jnp.zeros((round_up(kpad, 8) - kpad, 128), jnp.float32)
+    totals = jnp.transpose(jnp.concatenate([centered_sum - dropped, fill], 0))
 
     place = lax.broadcasted_iota(jnp.int32, (kpad, wide), 1)
     tail = jnp.zeros((kpad, 128), jnp.float32)
@@ -213,27 +214,45 @@
             field_copy(step).wait()
 
         got = recv[step]
-        acc[0 : kcount * rows, :] += jnp.dot(
-            win[step, :, :t_dev], got, preferred_element_type=jnp.float32
-        )
+        add_products(step, 0, count)
+        add_sums(got)
+        return carry
+
+    count = kcount * rows
+
+    def add_products(step, begin, end):
+        acc[begin:end, :] += jnp.dot(
+            win[step, begin:end, :t_dev], recv[step], preferred_element_type=jnp.float32
+        )
+
+    def add_sums(got):
         value = got.astype(jnp.float32)
         acc[kcount * rows : kcount * rows + 1, :] += jnp.sum(value, 0, keepdims=True)
         acc[kcount * rows + 1 : kcount * rows + 2, :] += jnp.sum(value * value, 0, keepdims=True)
-        return carry
 
     lax.fori_loop(0, chips, window_body, 0)
-    lax.fori_loop(0, chips, source_body, 0)
-    swap = pltpu.make_async_remote_copy(
-        src_ref=acc,
-        dst_ref=acc_in,
-        send_sem=last_send.at[1],
-        recv_sem=last_recv.at[1],
-        device_id=(partner,),
-        device_id_type=MESH,
-    )
-    swap.start()
-    swap.wait()
-    count = kcount * rows
+    lax.fori_loop(0, chips - 1, source_body, 0)
+
+    def swap(place, begin, end):
+        return pltpu.make_async_remote_copy(
+            src_ref=acc.at[pl.ds(begin, end - begin)],
+            dst_ref=acc_in.at[pl.ds(begin, end - begin)],
+            send_sem=last_send.at[place],
+            recv_sem=last_recv.at[place],
+            device_id=(partner,),
+            device_id_type=MESH,
+        )
+
+    middle = kcount // 2 * rows
+    field_copy(chips - 1).wait()
+    add_sums(recv[chips - 1])
+    swaps = [swap(1, count, count + 8), swap(2, 0, middle), swap(3, middle, count)]
+    swaps[0].start()
+    add_products(chips - 1, 0, middle)
+    swaps[1].start()
+    add_products(chips - 1, middle, count)
+    swaps[2].start()
+    swaps[0].wait()
     half = cells // 2
 
     def mine(begin, end):
@@ -248,6 +267,10 @@
     lag = lag_ref[...]
     row = lax.broadcasted_iota(jnp.int32, (rows, lag.shape[1]), 0)
     for k in range(kcount):
+        if k == 0:
+            swaps[1].wait()
+        if k == kcount // 2:
+            swaps[2].wait()
         numer = mine(k * rows, (k + 1) * rows) - mean_x * totals[0:rows, k : k + 1]
         value = numer / (inner * outer[k : k + 1]) * mask
         chosen = jnp.where(row == lag + (offset_ref[k] + MAXLAG), 1.0, 0.0)
@@ -264,7 +287,7 @@
     t_dev, cells_all = field.shape
     devices = lax.axis_size("tm")
     kcount = index.shape[1]
-    kpad = round_up(kcount, 16)
+    kpad = kcount
     lanes = round_up(t_dev, 128)
     rows = round_up(PLACES, 16)
     chips = devices // 2
@@ -276,6 +299,9 @@
     sizes = (devices, t_dev, kcount, kpad, rows, low)
     dma = pltpu.SemaphoreType.DMA
     f32 = jnp.float32
+    held = 4 * cells_all * t_dev + 4 * devices * round_up(kcount, 8) * lanes
+    held += 2 * chips * kcount * rows * lanes + 8 * (kcount * rows + 8) * cells
+    limit = held + 4 * 1024 * 1024
     vmem = pl.BlockSpec(memory_space=pltpu.VMEM)
     maps = pl.pallas_call(
         functools.partial(kernel, sizes),
@@ -302,8 +328,8 @@
             dma((high,)),
             dma((low,)),
             dma((low,)),
-            dma((2,)),
-            dma((2,)),
+            dma((4,)),
+            dma((4,)),
             dma((3,)),
         ],
         compiler_params=pltpu.CompilerParams(

time: 44.3 us -> 44.2 us (level)
  no operation moved by 1% of the time
where the time goes in v3:
time: 44.2 us; the launch traced here: 44 us
  Pallas kernels  42.3 us (96%)
  local copies, waits for them, and re-layouts  1.72 us (4%)
    pallas_call x1, Pallas kernels, shards(): pl.pallas_call(functools.partial(kernel, sizes), out_shape=jax.ShapeDtype...  42.3 us
    unnamed x1, local copies, waits for them, and re-layouts  1.72 us

profile of v3, /device:TPU:9, one launch (start us, length us, event | category | flops | bytes accessed | tf_op | source)
XLA Modules:
  0.0 44.0 jit_solution(1845498674088280262)
XLA Ops:
  0.0 42.3 %shard_map.55 = f32[10,64,61]{2,1,0:T(8,128)} custom-call(bf16[336,2048]{1,0:T(8,128)(2,1)} %field_hbm.1, f32[10,336]{1,0:T(8,128)} %bitcast.5, s32[1,61]{1,0:T(1,128)} %bitcast.6, s32[10]{0:T(128)} %offset_ref.1, s32[1,64]{1,0:T(1,128)} %bitcast.7), custom_call_target="tpu_custom_call" | custom-call | tf_op jit(solution)/shard_map/pallas_call | solution.py:306
  42.3 1.7 %copy.7 = f32[64,10,61]{2,0,1:T(8,128)} copy(f32[64,10,61]{2,0,1:T(8,128)} %bitcast.4) | data formatting | bytes 312320
